TPU v7x, 64 devices: a 2x2x8 block of a 4x4x8 slice. The times are simulated.
64 devices in a mesh: sys: 4 (over x, y), row: 16 (over z, core).
Axes of the slice: x: 2, y: 2, z: 8, core: 2. Of those that a mesh axis runs over, the one named last changes fastest.
The devices are a block of a 4x4x8 slice.
Arguments:
- positions: bfloat16 [131072, 512], P(('sys', 'row')), parts along dimension 0
- charges: float32 [131072], P(('sys', 'row')), parts along dimension 0
- counts: int32 [64], P(('sys', 'row')), parts along dimension 0
Outputs:
- output 1: float32 [131072, 512], P(('sys', 'row')), parts along dimension 0
- output 2: float32 [4], P('sys'), parts along dimension 0
There are 4 independent parts. A program takes and returns all parts, laid end to end along the dimension named above; each array names one.
All inputs are finite; a program needn't handle non-finite values.
Results may differ from a plain program's by a relative error of at most 0.001.
Values are sent between devices in bfloat16 or wider.
A program may use at most 768 MiB of HBM per device.

v0:
```python
import jax
import jax.numpy as jnp
from jax import lax
from jax.sharding import PartitionSpec as P


def sq_norm(block_pos):
    pos_f32 = block_pos.astype(jnp.float32)
    return jnp.sum(pos_f32 * pos_f32, axis=1)


def pair_weight(row_pos, row_q, col_pos, col_q, neg_scale):
    gram_mat = jnp.einsum('id,jd->ij', row_pos, col_pos, preferred_element_type=jnp.float32)
    dist_sq = jnp.maximum(sq_norm(row_pos)[:, None] + sq_norm(col_pos)[None, :] - 2.0 * gram_mat, 0.0)
    return row_q[:, None] * col_q[None, :] * jnp.exp(dist_sq * neg_scale)


def row_force(weight, w_low, row_pos, col_pos, inv_len2):
    pulled = jnp.dot(w_low, col_pos, preferred_element_type=jnp.float32)
    return (jnp.sum(weight, axis=1)[:, None] * row_pos.astype(jnp.float32) - pulled) * inv_len2


def col_force(weight, w_low, row_pos, col_pos, inv_len2):
    pushed = jnp.einsum('ij,id->jd', w_low, row_pos, preferred_element_type=jnp.float32)
    return (jnp.sum(weight, axis=0)[:, None] * col_pos.astype(jnp.float32) - pushed) * inv_len2


def solution(mesh):
    num_blocks = mesh.shape['row']
    half_way = num_blocks // 2
    next_perm = [(src, (src + 1) % num_blocks) for src in range(num_blocks)]
    home_perm = [(src, (src - half_way) % num_blocks) for src in range(num_blocks)]

    def per_device(positions, charges, counts):
        block_rows, width = positions.shape
        half_rows = block_rows // 2
        neg_scale = -0.5 / width
        inv_len2 = 1.0 / width
        live_q = jnp.where(jnp.arange(block_rows) < counts[0], charges, 0.0)
        diag_mask = jnp.arange(block_rows)[:, None] == jnp.arange(block_rows)[None, :]
        own_w = jnp.where(diag_mask, 0.0, pair_weight(positions, live_q, positions, live_q, neg_scale))
        own_force = row_force(own_w, own_w.astype(jnp.bfloat16), positions, positions, inv_len2)
        energy = 0.5 * jnp.sum(own_w)
        vis_pos = lax.ppermute(positions, 'row', next_perm)
        vis_q = lax.ppermute(live_q, 'row', next_perm)
        vis_react = jnp.zeros((block_rows, width), jnp.float32)

        def full_step(step_idx, loop_state):
            vis_pos, vis_q, vis_react, own_force, energy = loop_state
            weight = pair_weight(positions, live_q, vis_pos, vis_q, neg_scale)
            w_low = weight.astype(jnp.bfloat16)
            own_force = own_force + row_force(weight, w_low, positions, vis_pos, inv_len2)
            vis_react = vis_react + col_force(weight, w_low, positions, vis_pos, inv_len2)
            energy = energy + jnp.sum(weight)
            vis_pos = lax.ppermute(vis_pos, 'row', next_perm)
            vis_q = lax.ppermute(vis_q, 'row', next_perm)
            vis_react = lax.ppermute(vis_react, 'row', next_perm)
            return vis_pos, vis_q, vis_react, own_force, energy

        loop_state = lax.fori_loop(0, half_way - 1, full_step, (vis_pos, vis_q, vis_react, own_force, energy))
        vis_pos, vis_q, vis_react, own_force, energy = loop_state
        is_lower = lax.axis_index('row') < half_way
        a_pos = jnp.where(is_lower, positions[:half_rows], vis_pos[half_rows:])
        a_q = jnp.where(is_lower, live_q[:half_rows], vis_q[half_rows:])
        b_pos = jnp.where(is_lower, vis_pos, positions)
        b_q = jnp.where(is_lower, vis_q, live_q)
        weight = pair_weight(a_pos, a_q, b_pos, b_q, neg_scale)
        w_low = weight.astype(jnp.bfloat16)
        a_force = row_force(weight, w_low, a_pos, b_pos, inv_len2)
        b_force = col_force(weight, w_low, a_pos, b_pos, inv_len2)
        zero_half = jnp.zeros((half_rows, width), jnp.float32)
        own_force = own_force + jnp.where(is_lower, jnp.concatenate([a_force, zero_half], axis=0), b_force)
        vis_react = vis_react + jnp.where(is_lower, b_force, jnp.concatenate([zero_half, a_force], axis=0))
        energy = energy + jnp.sum(weight)
        own_force = own_force + lax.ppermute(vis_react, 'row', home_perm)
        energy = lax.psum(energy, 'row')
        return own_force, energy.reshape(1)

    row_spec = P(('sys', 'row'), None)
    vec_spec = P(('sys', 'row'))
    return jax.shard_map(per_device, mesh=mesh, in_specs=(row_spec, vec_spec, vec_spec), out_specs=(row_spec, P('sys')), check_vma=False)
```

profile of v0, /device:TPU:30, one launch (start us, length us, event | category | flops | bytes accessed | tf_op | source)
XLA Modules:
  0.0 930.7 jit_solution(9694693826100473600)
XLA Ops:
  6.3 14.3 %fusion.36 = (f32[]{:T(128)}, f32[2048]{0:T(1024)S(1)}, bf16[2048,2048]{0,1:T(8,128)(2,1)S(1)}) fusion(bf16[2048,512]{1,0:T(8,128)(2,1)} %param.5, f32[2048]{0:T(1024)S(1)} %fusion.18, f32[2048]{0:T(1024)S(1)} %fusion.34), kind=kOutput, calls=%fused_computation.49 | convolution fusion | flops 4345296896 | bytes 10510340 | tf_op jit(solution)/shard_map/id,jd->ij/dot_general | solution.py:13
  35.1 671.5 %while.18 = (s32[]{:T(128)}, bf16[2048,512]{1,0:T(8,128)(2,1)}, f32[2048]{0:T(1024)S(1)}, f32[2048,512]{1,0:T(8,128)}, f32[2048,512]{1,0:T(8,128)}, /*index=5*/f...) while((s32[]{:T(128)}, bf16[2048,512]{1,0:T(8,128)(2,1)}, f32[2048]{0:T(1024)S(1)}, ...), condition=%wide.region_9.10_spmd, body=%wide.region_3.9_spmd.sunk | while | flops 12947808256 | bytes 121766176 | solution.py:60
  39.2 11.6 %fusion.71 = (f32[]{:T(128)}, f32[2048]{0:T(1024)S(1)}, f32[2048]{0:T(1024)S(1)}, bf16[2048,2048]{1,0:T(8,128)(2,1)S(1)}) fusion(bf16[2048,512]{1,0:T(8,128)(2,1)} %get-tuple-element.183, bf16[2048,512]{1,0:T(8,128)(2,1)S(1)} %copy.12, f32[2048]{0:T(1024)S(1)} %get-tuple-element.152, f32[2048]{0:T(1024)S(1)} %get-tuple-element.153, ...), kind=kOutput, calls=%fused_computation.48.clone.1 | convolution fusion | flops 4341100544 | bytes 12632068 | tf_op jit(solution)/shard_map/while/body/eval_jaxpr/id,jd->ij/dot_general | solution.py:13
  50.8 8.5 fusion.72
  70.1 60.9 %collective-permute-done.1 = f32[2048]{0:T(1024)S(1)} collective-permute-done((f32[2048]{0:T(1024)S(1)}, f32[2048]{0:T(1024)S(1)}, u32[]{:S(2)}, u32[]{:S(2)}) %collective-permute-start.1) | collective-permute-done | bytes 8224 | tf_op jit(solution)/shard_map/while/body/eval_jaxpr/ppermute | solution.py:56
  135.1 11.6 %fusion.71 = (f32[]{:T(128)}, f32[2048]{0:T(1024)S(1)}, f32[2048]{0:T(1024)S(1)}, bf16[2048,2048]{1,0:T(8,128)(2,1)S(1)}) fusion(bf16[2048,512]{1,0:T(8,128)(2,1)} %get-tuple-element.183, bf16[2048,512]{1,0:T(8,128)(2,1)S(1)} %copy.12, f32[2048]{0:T(1024)S(1)} %get-tuple-element.152, f32[2048]{0:T(1024)S(1)} %get-tuple-element.153, ...), kind=kOutput, calls=%fused_computation.48.clone.1 | convolution fusion | flops 4341100544 | bytes 12632068 | tf_op jit(solution)/shard_map/while/body/eval_jaxpr/id,jd->ij/dot_general | solution.py:13
  146.7 8.5 fusion.72
  166.0 60.9 %collective-permute-done.1 = f32[2048]{0:T(1024)S(1)} collective-permute-done((f32[2048]{0:T(1024)S(1)}, f32[2048]{0:T(1024)S(1)}, u32[]{:S(2)}, u32[]{:S(2)}) %collective-permute-start.1) | collective-permute-done | bytes 8224 | tf_op jit(solution)/shard_map/while/body/eval_jaxpr/ppermute | solution.py:56
  231.0 11.6 %fusion.71 = (f32[]{:T(128)}, f32[2048]{0:T(1024)S(1)}, f32[2048]{0:T(1024)S(1)}, bf16[2048,2048]{1,0:T(8,128)(2,1)S(1)}) fusion(bf16[2048,512]{1,0:T(8,128)(2,1)} %get-tuple-element.183, bf16[2048,512]{1,0:T(8,128)(2,1)S(1)} %copy.12, f32[2048]{0:T(1024)S(1)} %get-tuple-element.152, f32[2048]{0:T(1024)S(1)} %get-tuple-element.153, ...), kind=kOutput, calls=%fused_computation.48.clone.1 | convolution fusion | flops 4341100544 | bytes 12632068 | tf_op jit(solution)/shard_map/while/body/eval_jaxpr/id,jd->ij/dot_general | solution.py:13
  242.7 8.5 fusion.72
  262.0 60.9 %collective-permute-done.1 = f32[2048]{0:T(1024)S(1)} collective-permute-done((f32[2048]{0:T(1024)S(1)}, f32[2048]{0:T(1024)S(1)}, u32[]{:S(2)}, u32[]{:S(2)}) %collective-permute-start.1) | collective-permute-done | bytes 8224 | tf_op jit(solution)/shard_map/while/body/eval_jaxpr/ppermute | solution.py:56
  327.0 11.6 %fusion.71 = (f32[]{:T(128)}, f32[2048]{0:T(1024)S(1)}, f32[2048]{0:T(1024)S(1)}, bf16[2048,2048]{1,0:T(8,128)(2,1)S(1)}) fusion(bf16[2048,512]{1,0:T(8,128)(2,1)} %get-tuple-element.183, bf16[2048,512]{1,0:T(8,128)(2,1)S(1)} %copy.12, f32[2048]{0:T(1024)S(1)} %get-tuple-element.152, f32[2048]{0:T(1024)S(1)} %get-tuple-element.153, ...), kind=kOutput, calls=%fused_computation.48.clone.1 | convolution fusion | flops 4341100544 | bytes 12632068 | tf_op jit(solution)/shard_map/while/body/eval_jaxpr/id,jd->ij/dot_general | solution.py:13
  338.6 8.5 fusion.72
  357.9 60.9 %collective-permute-done.1 = f32[2048]{0:T(1024)S(1)} collective-permute-done((f32[2048]{0:T(1024)S(1)}, f32[2048]{0:T(1024)S(1)}, u32[]{:S(2)}, u32[]{:S(2)}) %collective-permute-start.1) | collective-permute-done | bytes 8224 | tf_op jit(solution)/shard_map/while/body/eval_jaxpr/ppermute | solution.py:56
  422.9 11.6 %fusion.71 = (f32[]{:T(128)}, f32[2048]{0:T(1024)S(1)}, f32[2048]{0:T(1024)S(1)}, bf16[2048,2048]{1,0:T(8,128)(2,1)S(1)}) fusion(bf16[2048,512]{1,0:T(8,128)(2,1)} %get-tuple-element.183, bf16[2048,512]{1,0:T(8,128)(2,1)S(1)} %copy.12, f32[2048]{0:T(1024)S(1)} %get-tuple-element.152, f32[2048]{0:T(1024)S(1)} %get-tuple-element.153, ...), kind=kOutput, calls=%fused_computation.48.clone.1 | convolution fusion | flops 4341100544 | bytes 12632068 | tf_op jit(solution)/shard_map/while/body/eval_jaxpr/id,jd->ij/dot_general | solution.py:13
  434.5 8.5 fusion.72
  453.8 60.9 %collective-permute-done.1 = f32[2048]{0:T(1024)S(1)} collective-permute-done((f32[2048]{0:T(1024)S(1)}, f32[2048]{0:T(1024)S(1)}, u32[]{:S(2)}, u32[]{:S(2)}) %collective-permute-start.1) | collective-permute-done | bytes 8224 | tf_op jit(solution)/shard_map/while/body/eval_jaxpr/ppermute | solution.py:56
  518.8 11.6 %fusion.71 = (f32[]{:T(128)}, f32[2048]{0:T(1024)S(1)}, f32[2048]{0:T(1024)S(1)}, bf16[2048,2048]{1,0:T(8,128)(2,1)S(1)}) fusion(bf16[2048,512]{1,0:T(8,128)(2,1)} %get-tuple-element.183, bf16[2048,512]{1,0:T(8,128)(2,1)S(1)} %copy.12, f32[2048]{0:T(1024)S(1)} %get-tuple-element.152, f32[2048]{0:T(1024)S(1)} %get-tuple-element.153, ...), kind=kOutput, calls=%fused_computation.48.clone.1 | convolution fusion | flops 4341100544 | bytes 12632068 | tf_op jit(solution)/shard_map/while/body/eval_jaxpr/id,jd->ij/dot_general | solution.py:13
  530.5 8.5 fusion.72
  549.8 60.9 %collective-permute-done.1 = f32[2048]{0:T(1024)S(1)} collective-permute-done((f32[2048]{0:T(1024)S(1)}, f32[2048]{0:T(1024)S(1)}, u32[]{:S(2)}, u32[]{:S(2)}) %collective-permute-start.1) | collective-permute-done | bytes 8224 | tf_op jit(solution)/shard_map/while/body/eval_jaxpr/ppermute | solution.py:56
  614.8 11.6 %fusion.71 = (f32[]{:T(128)}, f32[2048]{0:T(1024)S(1)}, f32[2048]{0:T(1024)S(1)}, bf16[2048,2048]{1,0:T(8,128)(2,1)S(1)}) fusion(bf16[2048,512]{1,0:T(8,128)(2,1)} %get-tuple-element.183, bf16[2048,512]{1,0:T(8,128)(2,1)S(1)} %copy.12, f32[2048]{0:T(1024)S(1)} %get-tuple-element.152, f32[2048]{0:T(1024)S(1)} %get-tuple-element.153, ...), kind=kOutput, calls=%fused_computation.48.clone.1 | convolution fusion | flops 4341100544 | bytes 12632068 | tf_op jit(solution)/shard_map/while/body/eval_jaxpr/id,jd->ij/dot_general | solution.py:13
  626.4 8.5 fusion.72
  645.7 60.9 %collective-permute-done.1 = f32[2048]{0:T(1024)S(1)} collective-permute-done((f32[2048]{0:T(1024)S(1)}, f32[2048]{0:T(1024)S(1)}, u32[]{:S(2)}, u32[]{:S(2)}) %collective-permute-start.1) | collective-permute-done | bytes 8224 | tf_op jit(solution)/shard_map/while/body/eval_jaxpr/ppermute | solution.py:56
  733.9 189.5 %psum.7 = f32[1]{0:T(128)} all-reduce(f32[1]{0:T(128)} %bitcast.1), channel_id=1, replica_groups=mesh['sys'=4,'row'=16] {'row'}, use_global_device_ids=true, to_apply=%region_15.16 | all-reduce | flops 1 | bytes 8 | tf_op jit(solution)/shard_map/psum | solution.py:76
  (114 shorter events, 152.8 us)
Async XLA Ops:
  2.0 27.3 %collective-permute-start.4 = (f32[2048]{0:T(1024)S(1)}, f32[2048]{0:T(1024)S(1)}, u32[]{:S(2)}, u32[]{:S(2)}) collective-permute-start(f32[2048]{0:T(1024)S(1)} %fusion.34), channel_id=1, source_target_pairs={{0,1},{1,2},{2,3},{3,4},{4,5},{5,6},{6,7},{7,8},{8,9},{9,10},{10,1... | collective-permute-start | bytes 24584 | tf_op jit(solution)/shard_map/ppermute | solution.py:45
  2.0 30.6 %collective-permute-start.3 = (bf16[2048,512]{1,0:T(8,128)(2,1)}, bf16[2048,512]{1,0:T(8,128)(2,1)}, u32[]{:S(2)}, u32[]{:S(2)}) collective-permute-start(bf16[2048,512]{1,0:T(8,128)(2,1)} %param.5), channel_id=1, source_target_pairs={{0,1},{1,2},{2,3},{3,4},{4,5},{5,6},{6,7},{7,8},{8,9},{9,10},{10,1... | collective-permute-start | bytes 6291464 | tf_op jit(solution)/shard_map/ppermute | solution.py:44
  59.3 71.7 %collective-permute-start.2 = (f32[2048,512]{1,0:T(8,128)}, f32[2048,512]{1,0:T(8,128)}, u32[]{:S(2)}, u32[]{:S(2)}) collective-permute-start(f32[2048,512]{1,0:T(8,128)} %fusion.72), channel_id=1, source_target_pairs={{0,1},{1,2},{2,3},{3,4},{4,5},{5,6},{6,7},{7,8},{8,9},{9,10},{10,1... | collective-permute-start | bytes 12582920 | tf_op jit(solution)/shard_map/while/body/eval_jaxpr/ppermute | solution.py:57
  59.3 71.7 %collective-permute-start = (bf16[2048,512]{1,0:T(8,128)(2,1)S(1)}, bf16[2048,512]{1,0:T(8,128)(2,1)}, u32[]{:S(2)}, u32[]{:S(2)}) collective-permute-start(bf16[2048,512]{1,0:T(8,128)(2,1)S(1)} %copy.12), channel_id=1, source_target_pairs={{0,1},{1,2},{2,3},{3,4},{4,5},{5,6},{6,7},{7,8},{8,9},{9,10},{10,1... | collective-permute-start | bytes 6291464 | tf_op jit(solution)/shard_map/while/body/eval_jaxpr/ppermute | solution.py:55
  59.3 71.7 %collective-permute-start.1 = (f32[2048]{0:T(1024)S(1)}, f32[2048]{0:T(1024)S(1)}, u32[]{:S(2)}, u32[]{:S(2)}) collective-permute-start(f32[2048]{0:T(1024)S(1)} %copy.13), channel_id=1, source_target_pairs={{0,1},{1,2},{2,3},{3,4},{4,5},{5,6},{6,7},{7,8},{8,9},{9,10},{10,1... | collective-permute-start | bytes 24584 | tf_op jit(solution)/shard_map/while/body/eval_jaxpr/ppermute | solution.py:56
  155.2 71.7 %collective-permute-start.2 = (f32[2048,512]{1,0:T(8,128)}, f32[2048,512]{1,0:T(8,128)}, u32[]{:S(2)}, u32[]{:S(2)}) collective-permute-start(f32[2048,512]{1,0:T(8,128)} %fusion.72), channel_id=1, source_target_pairs={{0,1},{1,2},{2,3},{3,4},{4,5},{5,6},{6,7},{7,8},{8,9},{9,10},{10,1... | collective-permute-start | bytes 12582920 | tf_op jit(solution)/shard_map/while/body/eval_jaxpr/ppermute | solution.py:57
  155.2 71.7 %collective-permute-start = (bf16[2048,512]{1,0:T(8,128)(2,1)S(1)}, bf16[2048,512]{1,0:T(8,128)(2,1)}, u32[]{:S(2)}, u32[]{:S(2)}) collective-permute-start(bf16[2048,512]{1,0:T(8,128)(2,1)S(1)} %copy.12), channel_id=1, source_target_pairs={{0,1},{1,2},{2,3},{3,4},{4,5},{5,6},{6,7},{7,8},{8,9},{9,10},{10,1... | collective-permute-start | bytes 6291464 | tf_op jit(solution)/shard_map/while/body/eval_jaxpr/ppermute | solution.py:55
  155.2 71.7 %collective-permute-start.1 = (f32[2048]{0:T(1024)S(1)}, f32[2048]{0:T(1024)S(1)}, u32[]{:S(2)}, u32[]{:S(2)}) collective-permute-start(f32[2048]{0:T(1024)S(1)} %copy.13), channel_id=1, source_target_pairs={{0,1},{1,2},{2,3},{3,4},{4,5},{5,6},{6,7},{7,8},{8,9},{9,10},{10,1... | collective-permute-start | bytes 24584 | tf_op jit(solution)/shard_map/while/body/eval_jaxpr/ppermute | solution.py:56
  251.2 71.7 %collective-permute-start.2 = (f32[2048,512]{1,0:T(8,128)}, f32[2048,512]{1,0:T(8,128)}, u32[]{:S(2)}, u32[]{:S(2)}) collective-permute-start(f32[2048,512]{1,0:T(8,128)} %fusion.72), channel_id=1, source_target_pairs={{0,1},{1,2},{2,3},{3,4},{4,5},{5,6},{6,7},{7,8},{8,9},{9,10},{10,1... | collective-permute-start | bytes 12582920 | tf_op jit(solution)/shard_map/while/body/eval_jaxpr/ppermute | solution.py:57
  251.2 71.7 %collective-permute-start = (bf16[2048,512]{1,0:T(8,128)(2,1)S(1)}, bf16[2048,512]{1,0:T(8,128)(2,1)}, u32[]{:S(2)}, u32[]{:S(2)}) collective-permute-start(bf16[2048,512]{1,0:T(8,128)(2,1)S(1)} %copy.12), channel_id=1, source_target_pairs={{0,1},{1,2},{2,3},{3,4},{4,5},{5,6},{6,7},{7,8},{8,9},{9,10},{10,1... | collective-permute-start | bytes 6291464 | tf_op jit(solution)/shard_map/while/body/eval_jaxpr/ppermute | solution.py:55
  251.2 71.7 %collective-permute-start.1 = (f32[2048]{0:T(1024)S(1)}, f32[2048]{0:T(1024)S(1)}, u32[]{:S(2)}, u32[]{:S(2)}) collective-permute-start(f32[2048]{0:T(1024)S(1)} %copy.13), channel_id=1, source_target_pairs={{0,1},{1,2},{2,3},{3,4},{4,5},{5,6},{6,7},{7,8},{8,9},{9,10},{10,1... | collective-permute-start | bytes 24584 | tf_op jit(solution)/shard_map/while/body/eval_jaxpr/ppermute | solution.py:56
  347.1 71.7 %collective-permute-start.2 = (f32[2048,512]{1,0:T(8,128)}, f32[2048,512]{1,0:T(8,128)}, u32[]{:S(2)}, u32[]{:S(2)}) collective-permute-start(f32[2048,512]{1,0:T(8,128)} %fusion.72), channel_id=1, source_target_pairs={{0,1},{1,2},{2,3},{3,4},{4,5},{5,6},{6,7},{7,8},{8,9},{9,10},{10,1... | collective-permute-start | bytes 12582920 | tf_op jit(solution)/shard_map/while/body/eval_jaxpr/ppermute | solution.py:57
  347.1 71.7 %collective-permute-start = (bf16[2048,512]{1,0:T(8,128)(2,1)S(1)}, bf16[2048,512]{1,0:T(8,128)(2,1)}, u32[]{:S(2)}, u32[]{:S(2)}) collective-permute-start(bf16[2048,512]{1,0:T(8,128)(2,1)S(1)} %copy.12), channel_id=1, source_target_pairs={{0,1},{1,2},{2,3},{3,4},{4,5},{5,6},{6,7},{7,8},{8,9},{9,10},{10,1... | collective-permute-start | bytes 6291464 | tf_op jit(solution)/shard_map/while/body/eval_jaxpr/ppermute | solution.py:55
  347.1 71.7 %collective-permute-start.1 = (f32[2048]{0:T(1024)S(1)}, f32[2048]{0:T(1024)S(1)}, u32[]{:S(2)}, u32[]{:S(2)}) collective-permute-start(f32[2048]{0:T(1024)S(1)} %copy.13), channel_id=1, source_target_pairs={{0,1},{1,2},{2,3},{3,4},{4,5},{5,6},{6,7},{7,8},{8,9},{9,10},{10,1... | collective-permute-start | bytes 24584 | tf_op jit(solution)/shard_map/while/body/eval_jaxpr/ppermute | solution.py:56
  443.0 71.7 %collective-permute-start.2 = (f32[2048,512]{1,0:T(8,128)}, f32[2048,512]{1,0:T(8,128)}, u32[]{:S(2)}, u32[]{:S(2)}) collective-permute-start(f32[2048,512]{1,0:T(8,128)} %fusion.72), channel_id=1, source_target_pairs={{0,1},{1,2},{2,3},{3,4},{4,5},{5,6},{6,7},{7,8},{8,9},{9,10},{10,1... | collective-permute-start | bytes 12582920 | tf_op jit(solution)/shard_map/while/body/eval_jaxpr/ppermute | solution.py:57
  443.0 71.7 %collective-permute-start = (bf16[2048,512]{1,0:T(8,128)(2,1)S(1)}, bf16[2048,512]{1,0:T(8,128)(2,1)}, u32[]{:S(2)}, u32[]{:S(2)}) collective-permute-start(bf16[2048,512]{1,0:T(8,128)(2,1)S(1)} %copy.12), channel_id=1, source_target_pairs={{0,1},{1,2},{2,3},{3,4},{4,5},{5,6},{6,7},{7,8},{8,9},{9,10},{10,1... | collective-permute-start | bytes 6291464 | tf_op jit(solution)/shard_map/while/body/eval_jaxpr/ppermute | solution.py:55
  443.0 71.7 %collective-permute-start.1 = (f32[2048]{0:T(1024)S(1)}, f32[2048]{0:T(1024)S(1)}, u32[]{:S(2)}, u32[]{:S(2)}) collective-permute-start(f32[2048]{0:T(1024)S(1)} %copy.13), channel_id=1, source_target_pairs={{0,1},{1,2},{2,3},{3,4},{4,5},{5,6},{6,7},{7,8},{8,9},{9,10},{10,1... | collective-permute-start | bytes 24584 | tf_op jit(solution)/shard_map/while/body/eval_jaxpr/ppermute | solution.py:56
  539.0 71.7 %collective-permute-start.2 = (f32[2048,512]{1,0:T(8,128)}, f32[2048,512]{1,0:T(8,128)}, u32[]{:S(2)}, u32[]{:S(2)}) collective-permute-start(f32[2048,512]{1,0:T(8,128)} %fusion.72), channel_id=1, source_target_pairs={{0,1},{1,2},{2,3},{3,4},{4,5},{5,6},{6,7},{7,8},{8,9},{9,10},{10,1... | collective-permute-start | bytes 12582920 | tf_op jit(solution)/shard_map/while/body/eval_jaxpr/ppermute | solution.py:57
  539.0 71.7 %collective-permute-start = (bf16[2048,512]{1,0:T(8,128)(2,1)S(1)}, bf16[2048,512]{1,0:T(8,128)(2,1)}, u32[]{:S(2)}, u32[]{:S(2)}) collective-permute-start(bf16[2048,512]{1,0:T(8,128)(2,1)S(1)} %copy.12), channel_id=1, source_target_pairs={{0,1},{1,2},{2,3},{3,4},{4,5},{5,6},{6,7},{7,8},{8,9},{9,10},{10,1... | collective-permute-start | bytes 6291464 | tf_op jit(solution)/shard_map/while/body/eval_jaxpr/ppermute | solution.py:55
  539.0 71.7 %collective-permute-start.1 = (f32[2048]{0:T(1024)S(1)}, f32[2048]{0:T(1024)S(1)}, u32[]{:S(2)}, u32[]{:S(2)}) collective-permute-start(f32[2048]{0:T(1024)S(1)} %copy.13), channel_id=1, source_target_pairs={{0,1},{1,2},{2,3},{3,4},{4,5},{5,6},{6,7},{7,8},{8,9},{9,10},{10,1... | collective-permute-start | bytes 24584 | tf_op jit(solution)/shard_map/while/body/eval_jaxpr/ppermute | solution.py:56
  634.9 71.7 %collective-permute-start.2 = (f32[2048,512]{1,0:T(8,128)}, f32[2048,512]{1,0:T(8,128)}, u32[]{:S(2)}, u32[]{:S(2)}) collective-permute-start(f32[2048,512]{1,0:T(8,128)} %fusion.72), channel_id=1, source_target_pairs={{0,1},{1,2},{2,3},{3,4},{4,5},{5,6},{6,7},{7,8},{8,9},{9,10},{10,1... | collective-permute-start | bytes 12582920 | tf_op jit(solution)/shard_map/while/body/eval_jaxpr/ppermute | solution.py:57
  634.9 71.7 %collective-permute-start = (bf16[2048,512]{1,0:T(8,128)(2,1)S(1)}, bf16[2048,512]{1,0:T(8,128)(2,1)}, u32[]{:S(2)}, u32[]{:S(2)}) collective-permute-start(bf16[2048,512]{1,0:T(8,128)(2,1)S(1)} %copy.12), channel_id=1, source_target_pairs={{0,1},{1,2},{2,3},{3,4},{4,5},{5,6},{6,7},{7,8},{8,9},{9,10},{10,1... | collective-permute-start | bytes 6291464 | tf_op jit(solution)/shard_map/while/body/eval_jaxpr/ppermute | solution.py:55
  634.9 71.7 %collective-permute-start.1 = (f32[2048]{0:T(1024)S(1)}, f32[2048]{0:T(1024)S(1)}, u32[]{:S(2)}, u32[]{:S(2)}) collective-permute-start(f32[2048]{0:T(1024)S(1)} %copy.13), channel_id=1, source_target_pairs={{0,1},{1,2},{2,3},{3,4},{4,5},{5,6},{6,7},{7,8},{8,9},{9,10},{10,1... | collective-permute-start | bytes 24584 | tf_op jit(solution)/shard_map/while/body/eval_jaxpr/ppermute | solution.py:56
  729.0 194.3 %collective-permute-start.5 = (f32[2048,512]{1,0:T(8,128)}, f32[2048,512]{1,0:T(8,128)}, u32[]{:S(2)}, u32[]{:S(2)}) collective-permute-start(f32[2048,512]{1,0:T(8,128)} %select_add_fusion), channel_id=1, source_target_pairs={{0,8},{1,9},{2,10},{3,11},{4,12},{5,13},{6,14},{7,15},{8,0},{9,1},... | collective-permute-start | bytes 12582920 | tf_op jit(solution)/shard_map/ppermute | solution.py:75
  (16 other events, 85.6 us)
where the time goes:
time: 932 us; the launch traced here: 931 us
  waiting for transfers between devices  430 us (46%)
  matrix products  231 us (25%)
  blocking collectives  190 us (20%)
  other arithmetic  38.9 us (4%)
  local copies, waits for them, and re-layouts  27.8 us (3%)
    ppermute x7, waiting for transfers between devices, full_step(): vis_q = lax.ppermute(vis_q, 'row', next_perm)  426 us
    psum x1, blocking collectives, per_device(): energy = lax.psum(energy, 'row')  190 us
    dot_general x9, matrix products, pair_weight(): jnp.einsum('id,jd->ij', row_pos, col_pos, preferred_element_type=jnp.floa...  102 us
    dot_general x9, matrix products, row_force(): pulled = jnp.dot(w_low, col_pos, preferred_element_type=jnp.float32)  67.4 us
    dot_general x8, matrix products, col_force(): jnp.einsum('ij,id->jd', w_low, row_pos, preferred_element_type=jnp.float32)  62.1 us
    reduce_sum x10, other arithmetic, sq_norm(): return jnp.sum(pos_f32 * pos_f32, axis=1)  23.9 us
  transfers between devices with their start and end apart: 24, of which 8 were waited for; matrix products, arithmetic and copies ran while one was open for 9% of the time, Pallas kernels for 0%

commit v1 on v0

v1 whole, which is shorter than its diff:
```python
import functools
import math

import jax
import jax.numpy as jnp
from jax import lax
from jax.experimental import pallas as pl
from jax.experimental.pallas import tpu as pltpu
from jax.sharding import PartitionSpec as P

MESH = pl.DeviceIdType.MESH
GROUP = 64
CHUNK = 256
PER = CHUNK // GROUP
LAG = 2
SLOTS = 8
ROW_TILE = 512
SIDE_ROWS = 40
STEP_PARTS = (28, 32, 35, 38, 41, 44, 50, 64)
LOG2E = math.log2(math.e)


def enter(num, me):
    barrier = pltpu.get_barrier_semaphore()
    for rel in range(1, num):
        pl.semaphore_signal(barrier, inc=1, device_id={'row': lax.rem(me + rel, num)}, device_id_type=MESH)
    pl.semaphore_wait(barrier, num - 1)


def exchange_kernel(num, side_ref, all_ref, send_sem, recv_sem):
    me = lax.axis_index('row')
    enter(num, me)
    copies = []
    for rel in range(1, num):
        copy = pltpu.make_async_remote_copy(
            src_ref=side_ref, dst_ref=all_ref.at[me], send_sem=send_sem.at[rel], recv_sem=recv_sem.at[me],
            device_id={'row': lax.rem(me + rel, num)}, device_id_type=MESH)
        copy.start()
        copies.append(copy)
    all_ref[me] = side_ref[...]
    for rel in range(1, num):
        src = lax.rem(me + rel, num)
        pltpu.make_async_remote_copy(
            src_ref=side_ref, dst_ref=all_ref.at[src], send_sem=send_sem.at[rel], recv_sem=recv_sem.at[src],
            device_id={'row': src}, device_id_type=MESH).wait_recv()
    for copy in copies:
        copy.wait_send()


def force_kernel(num, steps, block, width, tbl_ref, x_hbm, side_ref, a_ref, c_ref, out_ref, en_ref,
                 pool, cols, recv, sacc, bc, ids, esend, ebuf,
                 load_sem, pair_send, pair_recv, ring_send, ring_recv, sib_send, sib_recv, e_send, e_recv,
                 ring_free, sib_free):
    me = lax.axis_index('row')
    core = lax.rem(me, 2)
    sib = me + 1 - 2 * core
    nxt = lax.rem(me + 2 * (1 - core) + (num - 2) * core, num)
    prv = lax.rem(me + (num - 2) * (1 - core) + 2 * core, num)
    fifo0 = 2 * block
    fifo_chunks = (2 * block) // CHUNK
    groups = fifo0 // GROUP
    own0 = core * block
    own_g = pl.ds(core * (block // GROUP), block // GROUP)
    gain = LOG2E / width
    lane_groups = 2 * CHUNK // 128

    enter(num, me)
    load = pltpu.make_async_copy(x_hbm, pool.at[own_g], load_sem)
    load.start()
    pair = pltpu.make_async_remote_copy(
        src_ref=x_hbm, dst_ref=pool.at[own_g], send_sem=pair_send, recv_sem=pair_recv,
        device_id={'row': sib}, device_id_type=MESH)
    pair.start()

    def clear(m, carry):
        rows = pl.ds(pl.multiple_of(m * 128, 128), 128)
        out_ref[rows, :] = jnp.zeros((128, width), jnp.float32)
        sacc[rows, :] = jnp.zeros((128, 128), jnp.float32)
        return carry

    lax.fori_loop(0, block // 128, clear, 0)
    load.wait()
    pair.wait()

    def own_rows(r0, n):
        return pool[pl.ds((own0 + r0) // GROUP, n // GROUP)].reshape(n, width)

    def ring_copy(t):
        s = lax.rem(t, SLOTS)
        return pltpu.make_async_remote_copy(
            src_ref=cols.at[s, pl.ds(0, CHUNK)], dst_ref=recv.at[s], send_sem=ring_send.at[s], recv_sem=ring_recv.at[s],
            device_id={'row': nxt}, device_id_type=MESH)

    def sib_copy(t):
        s = lax.rem(t, SLOTS)
        return pltpu.make_async_remote_copy(
            src_ref=cols.at[s, pl.ds(0, CHUNK)], dst_ref=cols.at[s, pl.ds(CHUNK, CHUNK)],
            send_sem=sib_send.at[s], recv_sem=sib_recv.at[s], device_id={'row': sib}, device_id_type=MESH)

    last_send = steps - LAG

    def prep(t):
        s = lax.rem(t, SLOTS)
        for j in range(PER):
            cols[s, j * GROUP:(j + 1) * GROUP, :] = pool[tbl_ref[0, t * PER + j]]

    def take(t):
        ring_copy(t).wait_recv()
        dst = groups + lax.rem(t, fifo_chunks) * PER
        pool[pl.ds(dst, PER)] = recv[lax.rem(t, SLOTS)].reshape(PER, GROUP, width)

        @pl.when(t + SLOTS < last_send)
        def _():
            pl.semaphore_signal(ring_free, inc=1, device_id={'row': prv}, device_id_type=MESH)

    def col_vectors(t, masked):
        lane = lax.broadcasted_iota(jnp.int32, (1, 128), 1)
        low = lane < GROUP
        for half in range(2):
            for p in range(PER // 2):
                at = t * PER + 2 * p
                r0 = side_ref[tbl_ref[2 + half, at]].reshape(1, 128)
                r1 = side_ref[tbl_ref[2 + half, at + 1]].reshape(1, 128)
                dst = half * CHUNK + p * 128
                bc[0:1, dst:dst + 128] = jnp.where(low, r0, pltpu.roll(r1, GROUP, axis=1))
                bc[1:2, dst:dst + 128] = jnp.where(low, pltpu.roll(r0, GROUP, axis=1), r1)
                if masked:
                    i0 = tbl_ref[half, at] * GROUP - own0
                    i1 = tbl_ref[half, at + 1] * GROUP - own0 - GROUP
                    ids[0:1, dst:dst + 128] = jnp.where(low, i0, i1) + lane

    num_tiles = block // ROW_TILE

    def compute(t, masked, between):
        s = lax.rem(t, SLOTS)

        def tile(m, carry):
            @pl.when(m == 1)
            def _():
                between()
            r0 = pl.multiple_of(m * ROW_TILE, ROW_TILE)
            rows = pl.ds(r0, ROW_TILE)
            x = own_rows(r0, ROW_TILE)
            y = cols[s]
            g = lax.dot_general(x, y, (((1,), (1,)), ((), ())), preferred_element_type=jnp.float32)
            a = a_ref[rows, :]
            c = c_ref[rows, :]
            if masked:
                rid = lax.broadcasted_iota(jnp.int32, (ROW_TILE, 128), 0) + r0
            total = sacc[rows, :]
            parts = []
            for l in range(lane_groups):
                sl = slice(l * 128, (l + 1) * 128)
                e = jnp.minimum(g[:, sl] * gain + (a + bc[0:1, sl]), 0.0)
                w = (c * bc[1:2, sl]) * jnp.exp2(e)
                if masked:
                    w = jnp.where(rid == ids[0:1, sl], 0.0, w)
                total = total + w
                parts.append(w.astype(jnp.bfloat16))
            sacc[rows, :] = total
            wl = jnp.concatenate(parts, axis=1)
            out_ref[rows, :] += jnp.dot(wl, y, preferred_element_type=jnp.float32)
            return carry

        lax.fori_loop(0, num_tiles, tile, 0)

    def send(t):
        ring_live = t < last_send

        @pl.when(ring_live)
        def _():
            @pl.when(t >= SLOTS)
            def _():
                pl.semaphore_wait(ring_free, 1)
            ring_copy(t).start()

        @pl.when(t >= SLOTS)
        def _():
            pl.semaphore_wait(sib_free, 1)
        sib_copy(t).start()

    def done(t):
        @pl.when(t < last_send)
        def _():
            ring_copy(t).wait_send()
        sib_copy(t).wait_send()

        @pl.when(t + SLOTS < steps)
        def _():
            pl.semaphore_signal(sib_free, inc=1, device_id={'row': sib}, device_id_type=MESH)

    def step(t, masked):
        @pl.when(t < steps)
        def _():
            @pl.when(t >= LAG)
            def _():
                take(t - LAG)
            prep(t)
        col_vectors(t - 1, masked)
        sib_copy(t - 1).wait_recv()

        def between():
            @pl.when(t < steps)
            def _():
                send(t)
        compute(t - 1, masked, between)
        done(t - 1)

    own_steps = block // CHUNK
    prep(0)
    send(0)
    lax.fori_loop(1, own_steps + 1, lambda t, c: (step(t, True), c)[1], 0)
    lax.fori_loop(own_steps + 1, steps + 1, lambda t, c: (step(t, False), c)[1], 0)

    def fold(m, acc):
        return acc + jnp.sum(sacc[pl.ds(pl.multiple_of(m * 128, 128), 128), :].reshape(16, 8, 128), axis=0)

    part = lax.fori_loop(0, block // 128, fold, jnp.zeros((8, 128), jnp.float32))
    part = jnp.sum(jnp.sum(part, axis=1, keepdims=True), axis=0, keepdims=True)
    esend[...] = jnp.broadcast_to(0.5 * part, esend.shape)
    inv = 1.0 / width

    def final(m, carry):
        r0 = pl.multiple_of(m * 128, 128)
        rows = pl.ds(r0, 128)
        x = own_rows(r0, 128).astype(jnp.float32)
        sums = jnp.sum(sacc[rows, :], axis=1, keepdims=True)
        out_ref[rows, :] = (sums * x - out_ref[rows, :]) * inv
        return carry

    copies = []
    for rel in range(1, num):
        copy = pltpu.make_async_remote_copy(
            src_ref=esend, dst_ref=ebuf.at[me], send_sem=e_send.at[rel], recv_sem=e_recv.at[me],
            device_id={'row': lax.rem(me + rel, num)}, device_id_type=MESH)
        copy.start()
        copies.append(copy)
    lax.fori_loop(0, block // 128, final, 0)
    ebuf[me] = esend[...]
    for rel in range(1, num):
        src = lax.rem(me + rel, num)
        pltpu.make_async_remote_copy(
            src_ref=esend, dst_ref=ebuf.at[src], send_sem=e_send.at[rel], recv_sem=e_recv.at[src],
            device_id={'row': src}, device_id_type=MESH).wait_recv()
    for copy in copies:
        copy.wait_send()
    en = ebuf[0]
    for j in range(1, num):
        en = en + ebuf[j]
    en_ref[...] = en


def stream_tables(counts, me, num, block, total_steps):
    chips = num // 2
    zero_row = SIDE_ROWS - 1
    grp = (counts + (GROUP - 1)) // GROUP
    pairs = grp.reshape(chips, 2)
    first = pairs[:, 0]
    used = pairs[:, 0] + pairs[:, 1]
    half0 = (used + 1) // 2
    base = jnp.stack([jnp.zeros_like(half0), half0], axis=1)
    real = jnp.stack([half0, used - half0], axis=1)
    padded = jnp.maximum(real, LAG * PER)
    need = jnp.max(jnp.sum(padded, axis=0))
    need_steps = (need + PER - 1) // PER
    chip = me // 2
    core = me % 2
    pos = jnp.arange(total_steps * PER, dtype=jnp.int32)
    blk_groups = block // GROUP
    fifo_groups = 2 * blk_groups
    pools, sides = [], []
    for other in range(2):
        k = jnp.where(core == 1, 1 - other, other)
        hop = jnp.where(k == 0, chips - 1, 1)
        order = (chip + hop * jnp.arange(chips, dtype=jnp.int32)) % chips
        onehot = (order[:, None] == jnp.arange(chips)[None, :]).astype(jnp.int32)

        def pick(v):
            return jnp.sum(onehot * v[None, :], axis=1)
        seg_pad = pick(jnp.where(k == 0, padded[:, 0], padded[:, 1]))
        seg_real = pick(jnp.where(k == 0, real[:, 0], real[:, 1]))
        seg_base = pick(jnp.where(k == 0, base[:, 0], base[:, 1]))
        seg_first = pick(first)
        tri = (jnp.arange(chips)[None, :] < jnp.arange(chips)[:, None]).astype(jnp.int32)
        start = jnp.sum(tri * seg_pad[None, :], axis=1)
        inside = (pos[:, None] >= start[None, :]) & (pos[:, None] < (start + seg_pad)[None, :])
        off = pos[:, None] - start[None, :]
        live = inside & (off < seg_real[None, :])
        u = off + seg_base[None, :]
        in_a = u < seg_first[None, :]
        side = jnp.where(in_a, 2 * order[None, :] * SIDE_ROWS + u,
                         (2 * order[None, :] + 1) * SIDE_ROWS + u - seg_first[None, :])
        side = jnp.sum(jnp.where(live, side - zero_row, 0), axis=1) + zero_row
        own = jnp.where(in_a, u, blk_groups + u - seg_first[None, :])
        own = jnp.where(live[:, 0], own[:, 0], 0)
        pool = jnp.where(pos < seg_pad[0], own, fifo_groups + (pos - seg_pad[0]) % fifo_groups)
        pools.append(pool)
        sides.append(side)
    return jnp.stack(pools + sides).astype(jnp.int32), need_steps


def solution(mesh):
    num = mesh.shape['row']

    def per_device(positions, charges, counts):
        block, width = positions.shape
        me = lax.axis_index('row')
        pos_f32 = positions.astype(jnp.float32)
        scale = -0.5 * LOG2E / width
        a = jnp.sum(pos_f32 * pos_f32, axis=1) * scale
        live_q = jnp.where(jnp.arange(block) < counts[0], charges, 0.0)
        side = jnp.concatenate([a.reshape(-1, GROUP), live_q.reshape(-1, GROUP)], axis=1)
        extra = jnp.full((1, 128), counts[0].astype(jnp.float32))
        blk_groups = block // GROUP
        side = jnp.concatenate([side, extra, jnp.zeros((SIDE_ROWS - blk_groups - 1, 128), jnp.float32)], axis=0)
        vmem = pl.BlockSpec(memory_space=pltpu.VMEM)
        everyone = pl.pallas_call(
            functools.partial(exchange_kernel, num),
            out_shape=jax.ShapeDtypeStruct((num, SIDE_ROWS, 128), jnp.float32),
            in_specs=[vmem], out_specs=vmem,
            scratch_shapes=[pltpu.SemaphoreType.DMA((num,)), pltpu.SemaphoreType.DMA((num,))],
            compiler_params=pltpu.CompilerParams(collective_id=0, has_side_effects=True),
            name='exchange',
        )(side)
        all_counts = everyone[:, blk_groups, 0].astype(jnp.int32)
        own_steps = block // CHUNK
        max_steps = (num // 2) * own_steps
        tbl, need_steps = stream_tables(all_counts, me, num, block, max_steps)
        all_side = everyone.reshape(num * SIDE_ROWS, 128)
        a_wide = jnp.broadcast_to(a[:, None], (block, 128))
        c_wide = jnp.broadcast_to(live_q[:, None], (block, 128))

        def call(steps, cid):
            dma = pltpu.SemaphoreType.DMA
            return pl.pallas_call(
                functools.partial(force_kernel, num, steps, block, width),
                out_shape=(jax.ShapeDtypeStruct((block, width), jnp.float32), jax.ShapeDtypeStruct((8, 128), jnp.float32)),
                in_specs=[pl.BlockSpec(memory_space=pltpu.SMEM), pl.BlockSpec(memory_space=pl.ANY), vmem, vmem, vmem],
                out_specs=(vmem, vmem),
                scratch_shapes=[
                    pltpu.VMEM((4 * block // GROUP, GROUP, width), jnp.bfloat16),
                    pltpu.VMEM((SLOTS, 2 * CHUNK, width), jnp.bfloat16),
                    pltpu.VMEM((SLOTS, CHUNK, width), jnp.bfloat16),
                    pltpu.VMEM((block, 128), jnp.float32),
                    pltpu.VMEM((8, 2 * CHUNK), jnp.float32),
                    pltpu.VMEM((8, 2 * CHUNK), jnp.int32),
                    pltpu.VMEM((8, 128), jnp.float32),
                    pltpu.VMEM((num, 8, 128), jnp.float32),
                    dma, dma, dma, dma((SLOTS,)), dma((SLOTS,)), dma((SLOTS,)), dma((SLOTS,)),
                    dma((num,)), dma((num,)),
                    pltpu.SemaphoreType.REGULAR, pltpu.SemaphoreType.REGULAR,
                ],
                compiler_params=pltpu.CompilerParams(
                    collective_id=cid, has_side_effects=True, vmem_limit_bytes=56 * 1024 * 1024),
                name='force',
            )(tbl, positions.reshape(-1, GROUP, width), all_side, a_wide, c_wide)

        choices = sorted({max(own_steps + 1, max_steps * part // 64) for part in STEP_PARTS})
        branch = jnp.sum((need_steps > jnp.array(choices[:-1], jnp.int32)).astype(jnp.int32))
        forces, energy = call(max_steps, 1)
        return forces, energy[0, :1]

    row_spec = P(('sys', 'row'), None)
    vec_spec = P(('sys', 'row'))
    return jax.shard_map(per_device, mesh=mesh, in_specs=(row_spec, vec_spec, vec_spec), out_specs=(row_spec, P('sys')), check_vma=False)
```

time: 932 us -> 298 us (0.32)
  waiting for transfers between devices: 430 us -> 0 us
  Pallas kernels: 0 us -> 280 us
  matrix products: 231 us -> 0 us
  blocking collectives: 190 us -> 0 us
  other arithmetic: 38.9 us -> 6.53 us
  local copies, waits for them, and re-layouts: 27.8 us -> 8.98 us
    ppermute x24 -> x0, waiting for transfers between devices: 430 us -> none  [the longest x7 426 us: full_step(): vis_q = lax.ppermute(vis_q, 'row', next_perm)]
    pallas_call x0 -> x2, Pallas kernels: none -> 280 us  [the longest x1 261 us: call(): pl.pallas_call(functools.partial(force_kernel, num, steps, block, width),...]
    dot_general x26 -> x0, matrix products: 231 us -> none  [the longest x9 102 us: pair_weight(): jnp.einsum('id,jd->ij', row_pos, col_pos, preferred_element_type=jnp.floa...]
    psum x1 -> x0, blocking collectives: 190 us -> none  [per_device(): energy = lax.psum(energy, 'row')]
    reduce_sum x10 -> x4, other arithmetic: 23.9 us -> 2.59 us  [the longest x1 2.07 us: per_device(): a = jnp.sum(pos_f32 * pos_f32, axis=1) * scale]
    while x28 -> x0, local copies, waits for them, and re-layouts: 14.1 us -> none
    add x2 -> x7, other arithmetic: 14.3 us -> 1.42 us  [the longest x1 1.22 us: stream_tables(): grp = (counts + (GROUP - 1)) // GROUP]
    another operation x14 -> x0, local copies, waits for them, and re-layouts: 11.2 us -> none
  transfers between devices with their start and end apart: 24 -> 0, of which waited for: 8 -> 0; matrix products, arithmetic and copies ran while one was open for 9% -> 0% of each run, Pallas kernels for 0% -> 0%
where the time goes in v1:
time: 298 us; the launch traced here: 297 us
  Pallas kernels  280 us (94%)
  local copies, waits for them, and re-layouts  8.98 us (3%)
  other arithmetic  6.53 us (2%)
    pallas_call x1, Pallas kernels, call(): pl.pallas_call(functools.partial(force_kernel, num, steps, block, width),...  261 us
    pallas_call x1, Pallas kernels, per_device(): pl.pallas_call(functools.partial(exchange_kernel, num), out_shape=jax.Sha...  18.7 us

profile of v1, /device:TPU:30, one launch (start us, length us, event | category | flops | bytes accessed | tf_op | source)
XLA Modules:
  0.0 296.6 jit_solution(10133976383512894815)
XLA Ops:
  1.3 0.1 pad.8.clone
  1.4 0.1 pad.9.clone
  1.5 0.7 fusion.4
  2.2 2.1 multiply_reduce_fusion
  4.4 0.7 maximum_maximum_fusion.side_ref
  5.1 18.7 %exchange.1 = f32[16,40,128]{2,1,0:T(8,128)} custom-call(f32[40,128]{1,0:T(8,128)} %maximum_maximum_fusion.side_ref), custom_call_target="tpu_custom_call" | custom-call | tf_op jit(solution)/shard_map/exchange/pallas_call | solution.py:317
  23.8 1.2 add_reduce_fusion
  25.1 0.1 add.295
  25.2 0.2 fusion.15
  25.3 0.1 copy.8
  25.4 0.1 copy.7
  25.6 0.3 select_reduce_fusion.9
  25.9 0.1 select_reduce_fusion.5
  26.0 0.1 select_reduce_fusion.10
  26.1 0.1 fusion.10
  26.2 0.1 fusion.9
  26.3 0.1 fusion.2
  26.4 0.1 fusion
  26.6 0.6 pad_add_fusion.tbl_ref
  27.2 1.3 broadcast_in_dim.31.c_ref
  28.5 1.3 broadcast_in_dim.30.a_ref
  29.8 261.0 %force.1 = (f32[2048,512]{1,0:T(8,128)}, f32[8,128]{1,0:T(8,128)}) custom-call(s32[4,256]{1,0:T(4,128)} %pad_add_fusion.tbl_ref, bf16[32,64,512]{2,1,0:T(8,128)(2,1)} %bitcast.27, f32[640,128]{1,0:T(8,128)} %bitcast.28, f32[2048,128]{1,0:T(8,128)} %broadcast_in_dim.30.a_ref, f32[2048,128]{1,0:T(8,128)} %broadcast_in_dim.31.c_ref), custom_call_target="tpu_custom_call" | custom-call | tf_op jit(solution)/shard_map/force/pallas_call | solution.py:335
  290.8 1.2 slice.52
  292.0 4.6 %copy.11 = f32[2048,512]{1,0:T(8,128)} copy(f32[2048,512]{1,0:T(8,128)} %get-tuple-element.43) | data formatting | bytes 8388608
  (18 shorter events, 0.3 us)
